TPU v7x, 32 devices: a whole 2x2x4 slice. The times are simulated.
32 devices in a mesh: node: 32 (over z, y, x, core).
Axes of the slice: x: 2, y: 2, z: 4, core: 2. Of those that a mesh axis runs over, the one named last changes fastest.
Arguments:
- labels: bfloat16 [131072, 512], P('node'), may hold values from -6 to 6
- seed_mask: int32 [131072], P('node'), may hold values 0 or 1
- band_w: bfloat16 [1024, 3, 128, 128], P('node'), may hold values from 0.0009994507 to 1
- far_block: int32 [32, 32, 2], P('node'), may hold values from 0 to 511
- far_tile: int32 [32, 32, 2], P('node'), may hold values from 0 to 31
- far_count: int32 [32, 32], P('node'), may hold values from 0 to 2, as said below
- far_w: bfloat16 [32, 32, 2, 8, 128], P('node'), may hold values from 0.049804688 to 2
Outputs:
- final_labels: bfloat16 [131072, 512], P('node')
- residual: float32 [2, 1024], P(None, 'node')
Inputs may be any that keep to these rules, and one draw needn't show every extreme that they name: `far_count`: in every draw at least one destination shard has all 2 slots live from every source shard; other counts vary from pair to pair.
All inputs are finite; a program needn't handle non-finite values. No bound on the sum of `seed_mask` on one device may be relied on, other than what follows from the above.
Results may differ from a plain program's by a relative error of at most 0.0027.
Values may be sent and summed in bfloat16 or wider, within the bound.
A program may use at most 128 MiB of HBM per device.

v0:
```python
import functools

import jax
import jax.numpy as jnp
from jax import lax
from jax.experimental import pallas as pl
from jax.experimental.pallas import tpu as pltpu
from jax.sharding import PartitionSpec as P

ITERS = 2
MESH = pl.DeviceIdType.MESH
ROWS = 32
GROUP = 16


def kernel(
    dims,
    labels_hbm, band_hbm, farw_hbm, req_ref, tile_ref, count_ref, seed_ref,
    out_ref, res_ref,
    cur0, cur1, band, farw, wide_t, onehot, placed, acc, far_a, far_b, inv, part,
    halo0, halo1, send0, send1, recv0, recv1, req_in, req_s,
    lab_sem, band_sem, farw_sem, smem_sem,
    req_send, req_recv, halo_send, halo_recv, blk_send, blk_recv,
):
    n, tiles, tile, slots, blk, classes = dims
    rows = tiles * tile
    lane = 128
    per = slots * blk
    far_rows = n * per
    me = lax.axis_index("node")
    right, left = lax.rem(me + 1, n), lax.rem(me + n - 1, n)
    cur = (cur0, cur1)
    halo, send, recv = (halo0, halo1), (send0, send1), (recv0, recv1)

    def groups(start, size):
        return pl.ds(start // GROUP, size // GROUP)

    def as_rows(value):
        return value.reshape(-1, classes)

    lab_copy = pltpu.make_async_copy(labels_hbm, cur0.at[groups(tile, rows)], lab_sem)
    band_copy = pltpu.make_async_copy(band_hbm, band, band_sem)
    farw_copy = pltpu.make_async_copy(farw_hbm, farw, farw_sem)
    lab_copy.start()
    farw_copy.start()
    band_copy.start()

    barrier = pltpu.get_barrier_semaphore()

    @pl.loop(1, n)
    def _(j):
        pl.semaphore_signal(barrier, inc=1, device_id=(lax.rem(me + j, n),), device_id_type=MESH)

    pl.semaphore_wait(barrier, n - 1)

    @pl.loop(1, n)
    def _(j):
        peer = lax.rem(me + j, n)
        pltpu.make_async_remote_copy(
            req_ref, req_in.at[me], req_send, req_recv,
            device_id=(peer,), device_id_type=MESH,
        ).start()

    def halo_copies(it, low, high):
        return (
            pltpu.make_async_remote_copy(
                high, halo[it].at[0], halo_send.at[it, 0], halo_recv.at[it, 0],
                device_id=(right,), device_id_type=MESH,
            ),
            pltpu.make_async_remote_copy(
                low, halo[it].at[1], halo_send.at[it, 1], halo_recv.at[it, 1],
                device_id=(left,), device_id_type=MESH,
            ),
        )

    halo_first = halo_copies(
        0, labels_hbm.at[groups(0, tile)], labels_hbm.at[groups(rows - tile, tile)]
    )
    for copy in halo_first:
        copy.start()

    req_in[me] = req_ref[...]
    lab_copy.wait()
    pltpu.make_async_copy(req_in.at[pl.ds(0, n - 1)], req_in.at[pl.ds(0, n - 1)], req_recv).wait()
    smem_copy = pltpu.make_async_copy(req_in, req_s, smem_sem)
    smem_copy.start()
    smem_copy.wait()

    def block_copy(it, j):
        peer = lax.rem(me + j, n)
        return pltpu.make_async_remote_copy(
            send[it].at[peer], recv[it].at[me], blk_send.at[it], blk_recv.at[it],
            device_id=(peer,), device_id_type=MESH,
        )

    def gathered(it, peer):
        halves = []
        for k in range(slots):
            wanted = req_s[peer, k, me]
            pair = cur[it][wanted // 2 + tile // GROUP].astype(jnp.float32)
            odd = jnp.full((blk, classes), wanted % 2, jnp.int32) == 1
            halves.append(jnp.where(odd, pair[blk:], pair[:blk]))
        return jnp.concatenate(halves, axis=0).astype(jnp.bfloat16)

    def exchange(it):
        @pl.loop(1, n)
        def _(j):
            peer = lax.rem(me + j, n)
            send[it][peer] = gathered(it, peer)

            @pl.when(j > 1)
            def _():
                block_copy(it, j - 1).start()

        recv[it][me] = gathered(it, me)
        block_copy(it, n - 1).start()

    def await_halo(it, copies):
        for copy in copies:
            copy.wait()
        cur[it][groups(0, tile)] = halo[it][0]
        cur[it][groups(rows + tile, tile)] = halo[it][1]

    def await_blocks(it):
        both = pl.ds(0, n - 1)
        pltpu.make_async_copy(send[it].at[both], send[it].at[both], blk_send.at[it]).wait()
        pltpu.make_async_copy(recv[it].at[both], recv[it].at[both], blk_recv.at[it]).wait()

    def band_pass(it, start, stop):
        zero = jnp.zeros((tile, tile), jnp.bfloat16)

        @pl.loop(start, stop)
        def _(p):
            first = [band[2 * p, o] for o in range(3)]
            second = [band[2 * p + 1, o] for o in range(3)]
            weights = jnp.concatenate(
                [jnp.concatenate(first + [zero], axis=1), jnp.concatenate([zero] + second, axis=1)],
                axis=0,
            )
            base = pl.multiple_of(p * (2 * tile), 2 * tile)
            acc[pl.ds(base, 2 * tile), :] = jnp.dot(
                weights,
                as_rows(cur[it][pl.ds(p * (2 * tile // GROUP), 4 * tile // GROUP)]),
                preferred_element_type=jnp.float32,
            )

    def far_pass(it, p, into):
        base = pl.multiple_of(p * (2 * tile), 2 * tile)
        into[...] = jnp.dot(
            placed[pl.ds(base, 2 * tile), :],
            recv[it][...].reshape(far_rows, classes),
            preferred_element_type=jnp.float32,
        )

    def finish(it, p, far):
        last = it == ITERS - 1
        target = out_ref if last else cur[1 - it]
        for half in range(2):
            total = jnp.zeros((8, lane), jnp.float32)
            for r in range(0, tile, ROWS):
                base = pl.multiple_of(p * (2 * tile) + half * tile + r, ROWS)
                here = pl.ds(base, ROWS)
                local = slice(half * tile + r, half * tile + r + ROWS)
                spread = [
                    acc[here, c : c + lane] + far[local, c : c + lane]
                    for c in range(0, classes, lane)
                ]
                squares = spread[0] * spread[0]
                for s in spread[1:]:
                    squares = squares + s * s
                mean = jnp.sum(squares, axis=1, keepdims=True) * (1.0 / classes)
                signed = inv[here, :]
                size = jnp.abs(signed)
                factor = size / jnp.maximum(size * jnp.sqrt(mean), 0.05)
                keep = signed < 0.0
                padded = pl.ds(
                    p * (2 * tile // GROUP) + (half * tile + r + tile) // GROUP, ROWS // GROUP
                )
                written = pl.ds(padded.start - tile // GROUP, padded.size) if last else padded
                for q, s in enumerate(spread):
                    where = slice(q * lane, (q + 1) * lane)
                    before = cur[it][padded, :, where].reshape(ROWS, lane).astype(jnp.float32)
                    fresh = jnp.where(keep, before, s * factor).astype(jnp.bfloat16)
                    target[written, :, where] = fresh.reshape(ROWS // GROUP, GROUP, lane)
                    change = jnp.abs(fresh.astype(jnp.float32) - before)
                    for i in range(0, ROWS, 8):
                        total = total + change[i : i + 8]
            part[2 * p + half] = total

    def prepare():
        wide_t[...] = farw[...].astype(jnp.float32).T
        tile_of = lax.broadcasted_iota(jnp.int32, (tiles, n), 0)
        block_of = lax.shift_right_logical(
            lax.broadcasted_iota(jnp.int32, (n, far_rows), 1), blk.bit_length() - 1
        )
        peer_of = lax.broadcasted_iota(jnp.int32, (n, far_rows), 0)
        table = jnp.zeros((tiles, far_rows), jnp.float32)
        for k in range(slots):
            target = jnp.where(count_ref[...] > k, tile_ref[k : k + 1, :], -1)
            chosen = (tile_of == target).astype(jnp.float32)
            spread = (block_of == peer_of * slots + k).astype(jnp.float32)
            table = table + jnp.dot(
                chosen.astype(jnp.bfloat16),
                spread.astype(jnp.bfloat16),
                preferred_element_type=jnp.float32,
            )
        onehot[...] = table

        @pl.loop(0, tiles)
        def _(t):
            base = pl.multiple_of(t * tile, tile)
            weights = wide_t[...] * onehot[pl.ds(t, 1), :]
            placed[pl.ds(base, tile), :] = weights.astype(jnp.bfloat16)
            total = band[t, 0].astype(jnp.float32)
            for o in range(1, 3):
                total = total + band[t, o].astype(jnp.float32)
            for c in range(0, far_rows, lane):
                total = total + weights[:, c : c + lane]
            degree = jnp.sum(total, axis=1, keepdims=True)
            seeded = jnp.broadcast_to(seed_ref[pl.ds(t, 1), :].astype(jnp.float32), (tile, tile)).T
            inverse = jnp.broadcast_to(1.0 / degree, (tile, tile))
            inv[pl.ds(base, tile), :] = jnp.where(seeded == 1.0, -inverse, inverse)

    pairs = tiles // 2
    copies = halo_first
    for it in range(ITERS):
        exchange(it)
        if it == 0:
            farw_copy.wait()
            band_copy.wait()
            prepare()
        band_pass(it, 1, pairs - 1)
        await_halo(it, copies)
        band_pass(it, 0, 1)
        band_pass(it, pairs - 1, pairs)
        await_blocks(it)

        last = it == ITERS - 1
        if not last:
            copies = halo_copies(
                it + 1, cur[it + 1].at[groups(tile, tile)], cur[it + 1].at[groups(rows, tile)]
            )

        def pair_at(i):
            return lax.rem(i + pairs - 1, pairs)

        far_pass(it, pair_at(0), far_a)

        @pl.loop(0, pairs // 2)
        def _(q):
            far_pass(it, pair_at(2 * q + 1), far_b)
            finish(it, pair_at(2 * q), far_a)
            far_pass(it, pair_at(2 * q + 2), far_a)
            finish(it, pair_at(2 * q + 1), far_b)
            if not last:

                @pl.when(q == 1)
                def _():
                    for copy in copies:
                        copy.start()

        sums = jnp.sum(part[...], axis=1)
        res_ref[it : it + 1, :] = jnp.sum(sums.T, axis=0, keepdims=True)

    both = pl.ds(0, n - 1)
    pltpu.make_async_copy(req_in.at[both], req_in.at[both], req_send).wait()


def body(labels, seed_mask, band_w, far_block, far_tile, far_count, far_w):
    rows, classes = labels.shape
    tiles, _, tile, _ = band_w.shape
    _, n, slots, blk, _ = far_w.shape
    lane = 128
    per = slots * blk
    dims = (n, tiles, tile, slots, blk, classes)
    vmem, anywhere = pltpu.VMEM, pl.BlockSpec(memory_space=pl.ANY)
    held = pl.BlockSpec(memory_space=pltpu.VMEM)
    dma = pltpu.SemaphoreType.DMA
    bf16, f32 = jnp.bfloat16, jnp.float32
    out, residual = pl.pallas_call(
        functools.partial(kernel, dims),
        out_shape=(
            pltpu.VMEM((rows // GROUP, GROUP, classes), bf16),
            jax.ShapeDtypeStruct((ITERS, tiles), f32),
        ),
        in_specs=[anywhere, anywhere, anywhere, held, held, held, held],
        out_specs=(held, held),
        scratch_shapes=[
            vmem(((rows + 2 * tile) // GROUP, GROUP, classes), bf16),
            vmem(((rows + 2 * tile) // GROUP, GROUP, classes), bf16),
            vmem(band_w.shape, bf16),
            vmem((n * per, tile), bf16),
            vmem((tile, n * per), f32),
            vmem((tiles, n * per), f32),
            vmem((rows, n * per), bf16),
            vmem((rows, classes), f32),
            vmem((2 * tile, classes), f32),
            vmem((2 * tile, classes), f32),
            vmem((rows, lane), f32),
            vmem((tiles, 8, lane), f32),
            vmem((2, tile // GROUP, GROUP, classes), bf16),
            vmem((2, tile // GROUP, GROUP, classes), bf16),
            vmem((n, per, classes), bf16),
            vmem((n, per, classes), bf16),
            vmem((n, per, classes), bf16),
            vmem((n, per, classes), bf16),
            vmem((n, slots, n), jnp.int32),
            pltpu.SMEM((n, slots, n), jnp.int32),
            dma, dma, dma, dma,
            dma, dma,
            dma((ITERS, 2)), dma((ITERS, 2)),
            dma((ITERS,)), dma((ITERS,)),
        ],
        compiler_params=pltpu.CompilerParams(
            collective_id=0, has_side_effects=True, vmem_limit_bytes=56 * 1024 * 1024
        ),
    )(
        labels.reshape(rows // GROUP, GROUP, classes),
        band_w,
        far_w.reshape(n * per, tile),
        far_block[0].T,
        far_tile[0].T,
        far_count,
        seed_mask.reshape(tiles, tile),
    )
    return out.reshape(rows, classes), residual


def solution(mesh):
    placed = (
        P("node", None),
        P("node"),
        P("node", None, None, None),
        P("node", None, None),
        P("node", None, None),
        P("node", None),
        P("node", None, None, None, None),
    )
    return jax.shard_map(
        body,
        mesh=mesh,
        in_specs=placed,
        out_specs=(P("node", None), P(None, "node")),
        check_vma=False,
    )
```

profile of v0, /device:TPU:29, one launch (start us, length us, event | category | flops | bytes accessed | tf_op | source)
XLA Modules:
  0.0 54.4 jit_solution(17920197537995960661)
XLA Ops:
  0.6 51.2 %shard_map.86 = (bf16[256,16,512]{2,1,0:T(8,128)(2,1)S(1)}, f32[2,32]{1,0:T(2,128)}) custom-call(bf16[256,16,512]{2,1,0:T(8,128)(2,1)} %bitcast.11, bf16[32,3,128,128]{3,2,1,0:T(8,128)(2,1)} %band_hbm.1, bf16[512,128]{1,0:T(8,128)(2,1)} %bitcast.12, s32[2,32]{1,0:T(2,128)} %bitcast.14, s32[2,32]{1,0:T(2,128)} %bitcast.15, s32[1,32]{1,0:T(1,128)} %count_ref.1, ...), custom_call_target="tpu_custom_call" | custom-call | tf_op jit(solution)/shard_map/pallas_call | solution.py:280
  51.8 0.0 copy-start
  51.8 2.0 %copy.11 = bf16[4096,512]{1,0:T(8,128)(2,1)} copy(bf16[4096,512]{1,0:T(8,128)(2,1)S(1)} %bitcast.10) | data formatting | bytes 8388608
  53.9 0.0 copy-done
  53.9 0.6 %copy.12 = f32[2,32]{1,0:T(2,128)} copy(f32[2,32]{1,0:T(2,128)S(1)} %copy-done) | data formatting | bytes 512
Async XLA Ops:
  51.8 2.0 %copy-start = (f32[2,32]{1,0:T(2,128)S(1)}, f32[2,32]{1,0:T(2,128)}, u32[]{:S(2)}) copy-start(f32[2,32]{1,0:T(2,128)} %get-tuple-element.11) | copy-start | bytes 772
where the time goes:
time: 54.7 us; the launch traced here: 54.4 us
  Pallas kernels  51.2 us (94%)
  local copies, waits for them, and re-layouts  2.58 us (5%)
  between operations  0.65 us (1%)
    pallas_call x1, Pallas kernels, body(): pl.pallas_call(functools.partial(kernel, dims), out_shape=(pltpu.VMEM((ro...  51.2 us
    unnamed x4, local copies, waits for them, and re-layouts  2.58 us

commit v1 on v0

v1 whole, which is shorter than its diff:
```python
import functools

import jax
import jax.numpy as jnp
from jax import lax
from jax.experimental import pallas as pl
from jax.experimental.pallas import tpu as pltpu
from jax.sharding import PartitionSpec as P

ITERS = 2
CHUNKS = 2
MESH = pl.DeviceIdType.MESH
ROWS = 32
GROUP = 16
SUB = 8
LANE = 128
WIDE = 256
FLOOR = 0.05
BAND_UNROLL = 7
FAR_UNROLL = 4
SEND_UNROLL = 4
SCALE_UNROLL = 16
PREP_UNROLL = 4


def kernel(
    dims,
    labels_hbm, band_hbm, farw_hbm, req_ref, tile_ref, count_ref, seed_ref,
    out_ref, res_ref,
    cur0, cur1, band, farw, wide_t, onehot, placed, acc, far_a, far_b, limit, kept, fac, part,
    halo0, halo1, send, recv, fac_out, fac_in, req_s,
    lab_sem, band_sem, farw_sem, smem_sem,
    req_send, req_recv, halo_send, halo_recv, blk_send, blk_recv, fac_send, fac_recv,
):
    n, tiles, tile, slots, blk, classes = dims
    rows = tiles * tile
    per = slots * blk
    far_rows = n * per
    width = classes // CHUNKS
    me = lax.axis_index("node")
    right, left = lax.rem(me + 1, n), lax.rem(me + n - 1, n)
    cur = (cur0, cur1)
    halo = (halo0, halo1)
    others = pl.ds(0, n - 1)
    pairs = tiles // 2

    def columns(c):
        return slice(c * width, (c + 1) * width)

    def groups(start, size):
        return pl.ds(start // GROUP, size // GROUP)

    def as_rows(value):
        return value.reshape(-1, value.shape[-1])

    barrier = pltpu.get_barrier_semaphore()

    @pl.loop(1, n)
    def _(j):
        pl.semaphore_signal(barrier, inc=1, device_id=(lax.rem(me + j, n),), device_id_type=MESH)

    lab_copy = pltpu.make_async_copy(labels_hbm, cur0.at[groups(tile, rows)], lab_sem)
    band_copy = pltpu.make_async_copy(band_hbm, band, band_sem)
    farw_copy = pltpu.make_async_copy(farw_hbm, farw, farw_sem)
    own_req = pltpu.make_async_copy(req_ref, req_s.at[me], smem_sem)
    own_req.start()
    farw_copy.start()
    band_copy.start()
    lab_copy.start()

    pl.semaphore_wait(barrier, n - 1)

    @pl.loop(1, n)
    def _(j):
        peer = lax.rem(me + j, n)
        pltpu.make_async_remote_copy(
            req_ref, req_s.at[me], req_send, req_recv,
            device_id=(peer,), device_id_type=MESH,
        ).start()

    def halo_copies(it, low, high):
        return (
            pltpu.make_async_remote_copy(
                high, halo[it].at[0], halo_send.at[it, 0], halo_recv.at[it, 0],
                device_id=(right,), device_id_type=MESH,
            ),
            pltpu.make_async_remote_copy(
                low, halo[it].at[1], halo_send.at[it, 1], halo_recv.at[it, 1],
                device_id=(left,), device_id_type=MESH,
            ),
        )

    halo_first = halo_copies(
        0, labels_hbm.at[groups(0, tile)], labels_hbm.at[groups(rows - tile, tile)]
    )
    for copy in halo_first:
        copy.start()

    def block_copy(it, c, j):
        peer = lax.rem(me + j, n)
        return pltpu.make_async_remote_copy(
            send.at[it, c, peer], recv.at[it, c, me], blk_send.at[it, c], blk_recv.at[it, c],
            device_id=(peer,), device_id_type=MESH,
        )

    def factor_copy(j):
        peer = lax.rem(me + j, n)
        return pltpu.make_async_remote_copy(
            fac_out.at[peer], fac_in.at[me], fac_send, fac_recv,
            device_id=(peer,), device_id_type=MESH,
        )

    def block_of(it, c, wanted):
        pair = cur[it][wanted // 2 + tile // GROUP, :, columns(c)].astype(jnp.float32)
        odd = jnp.full((blk, width), wanted % 2, jnp.int32) == 1
        return jnp.where(odd, pair[blk:], pair[:blk])

    def gathered(it, c, peer, raw):
        halves = []
        for k in range(slots):
            wanted = req_s[peer, k, me]
            if raw:
                seeded = jnp.concatenate([limit[wanted]] * (width // LANE), axis=1) < 0.0
                halves.append(
                    jnp.where(seeded, block_of(0, c, wanted), acc[wanted, :, columns(c)])
                )
            else:
                halves.append(block_of(it, c, wanted))
        return jnp.concatenate(halves, axis=0).astype(jnp.bfloat16)

    def send_all(fill, copy):
        @pl.loop(0, n // SEND_UNROLL)
        def _(q):
            for u in range(SEND_UNROLL):
                fill(lax.rem(me + q * SEND_UNROLL + u + 1, n))

            @pl.when(q > 0)
            def _():
                for u in range(SEND_UNROLL):
                    copy((q - 1) * SEND_UNROLL + u + 1).start()

    def send_rest(copy):
        for j in range(n - SEND_UNROLL + 1, n):
            copy(j).start()

    def exchange(it, c, raw=False):
        def fill(peer):
            send[it, c, peer] = gathered(it, c, peer, raw)

        def copy(j):
            return block_copy(it, c, j)

        send_all(fill, copy)
        recv[it, c, me] = send[it, c, me]
        send_rest(copy)

    diagonal = lax.broadcasted_iota(jnp.int32, (per, LANE), 0) == lax.broadcasted_iota(
        jnp.int32, (per, LANE), 1
    )

    def factors_for(peer):
        both = jnp.concatenate([fac[req_s[peer, k, me]] for k in range(slots)], axis=0)
        return jnp.sum(jnp.where(diagonal, both, 0.0), axis=0, keepdims=True)

    def exchange_factors():
        def fill(peer):
            fac_out[peer] = factors_for(peer)

        send_all(fill, factor_copy)
        fac_in[me] = fac_out[me]
        send_rest(factor_copy)

    def await_factors():
        pltpu.make_async_copy(fac_out.at[others], fac_out.at[others], fac_send).wait()
        pltpu.make_async_copy(fac_in.at[others], fac_in.at[others], fac_recv).wait()

    def await_halo(it, copies):
        for copy in copies:
            copy.wait()
        cur[it][groups(0, tile)] = halo[it][0]
        cur[it][groups(rows + tile, tile)] = halo[it][1]

    def await_blocks(it, c):
        out_going, coming = send.at[it, c, others], recv.at[it, c, others]
        pltpu.make_async_copy(out_going, out_going, blk_send.at[it, c]).wait()
        pltpu.make_async_copy(coming, coming, blk_recv.at[it, c]).wait()

    def scale_received(it, c):
        @pl.loop(0, n // SCALE_UNROLL)
        def _(q):
            for u in range(SCALE_UNROLL):
                s = q * SCALE_UNROLL + u
                column = jnp.sum(
                    jnp.where(diagonal, jnp.broadcast_to(fac_in[s], (per, LANE)), 0.0),
                    axis=1, keepdims=True,
                )
                value = recv[it, c, s].astype(jnp.float32) * column
                recv[it, c, s] = value.astype(jnp.bfloat16)

    def band_pairs(it, first, count):
        zero = jnp.zeros((tile, tile), jnp.bfloat16)
        for u in range(count):
            p = first + u
            upper = [band[2 * p, o] for o in range(3)]
            lower = [band[2 * p + 1, o] for o in range(3)]
            weights = jnp.concatenate(
                [
                    jnp.concatenate(upper + [zero], axis=1),
                    jnp.concatenate([zero] + lower, axis=1),
                ],
                axis=0,
            )
            total = jnp.dot(
                weights,
                as_rows(cur[it][pl.ds(p * (2 * tile // GROUP), 4 * tile // GROUP)]),
                preferred_element_type=jnp.float32,
            )
            acc[pl.ds(p * (2 * tile // SUB), 2 * tile // SUB)] = total.reshape(
                2 * tile // SUB, SUB, classes
            )

    inner = pairs - 2
    unroll = max(u for u in range(1, BAND_UNROLL + 1) if inner % u == 0)

    def band_inside(it):
        @pl.loop(0, inner // unroll)
        def _(q):
            band_pairs(it, q * unroll + 1, unroll)

    def band_edges(it):
        band_pairs(it, 0, 1)
        band_pairs(it, pairs - 1, 1)

    def far_dot(it, c, start, size):
        return jnp.dot(
            placed[pl.ds(pl.multiple_of(start, size), size), :],
            recv[it, c].reshape(far_rows, width),
            preferred_element_type=jnp.float32,
        )

    def far_add(it, c):
        size = 2 * tile

        @pl.loop(0, pairs // FAR_UNROLL)
        def _(q):
            for u in range(FAR_UNROLL):
                p = q * FAR_UNROLL + u
                here = pl.ds(p * (size // SUB), size // SUB)
                acc[here, :, columns(c)] += far_dot(it, c, p * size, size).reshape(
                    size // SUB, SUB, width
                )

    def far_pass(it, p, into):
        into[...] = far_dot(it, CHUNKS - 1, p * (2 * tile), 2 * tile)

    def finish(it, p, far):
        last = it == ITERS - 1
        target = out_ref if last else cur[1 - it]
        for half in range(2):
            total = jnp.zeros((8, LANE), jnp.float32)
            for r in range(0, tile, ROWS):
                row = p * (2 * tile) + half * tile + r
                here8 = pl.ds(row // SUB, ROWS // SUB)
                here16 = pl.ds(row // GROUP, ROWS // GROUP)
                padded = pl.ds(row // GROUP + tile // GROUP, ROWS // GROUP)
                local = slice(half * tile + r, half * tile + r + ROWS)
                spread = []
                for c in range(0, classes, WIDE):
                    value = acc[here8, :, c : c + WIDE].reshape(ROWS, WIDE)
                    start = (CHUNKS - 1) * width
                    if c >= start:
                        value = value + far[local, c - start : c - start + WIDE]
                    spread.append(value)
                squares = spread[0] * spread[0]
                for s in spread[1:]:
                    squares = squares + s * s
                mean = jnp.sum(squares, axis=1, keepdims=True) * (1.0 / classes)
                signed = limit[here8].reshape(ROWS, LANE)
                factor = jnp.minimum(lax.rsqrt(mean), jnp.abs(signed))
                if not last:
                    fac[here8] = jnp.where(signed < 0.0, 1.0, factor).reshape(
                        ROWS // SUB, SUB, LANE
                    )
                factor = jnp.concatenate([factor] * (WIDE // LANE), axis=1)
                keep = kept[here16] > 0.5
                written = here16 if last else padded
                moved = None
                for q, s in enumerate(spread):
                    where = slice(q * WIDE, (q + 1) * WIDE)
                    before = cur[it][padded, :, where]
                    scaled = (s * factor).reshape(ROWS // GROUP, GROUP, WIDE)
                    fresh = jnp.where(keep, before, scaled.astype(jnp.bfloat16))
                    target[written, :, where] = fresh
                    change = jnp.abs(fresh - before)
                    moved = change if moved is None else moved + change
                moved = moved.astype(jnp.float32).reshape(ROWS, WIDE)
                for i in range(0, ROWS, 8):
                    for c in range(0, WIDE, LANE):
                        total = total + moved[i : i + 8, c : c + LANE]
            part[2 * p + half] = total

    def prepare():
        wide_t[...] = farw[...].astype(jnp.float32).T
        tile_of = lax.broadcasted_iota(jnp.int32, (tiles, n), 0)
        block_of = lax.shift_right_logical(
            lax.broadcasted_iota(jnp.int32, (n, far_rows), 1), blk.bit_length() - 1
        )
        peer_of = lax.broadcasted_iota(jnp.int32, (n, far_rows), 0)
        table = jnp.zeros((tiles, far_rows), jnp.float32)
        for k in range(slots):
            target = jnp.where(count_ref[...] > k, tile_ref[k : k + 1, :], -1)
            chosen = (tile_of == target).astype(jnp.float32)
            spread = (block_of == peer_of * slots + k).astype(jnp.float32)
            table = table + jnp.dot(
                chosen.astype(jnp.bfloat16),
                spread.astype(jnp.bfloat16),
                preferred_element_type=jnp.float32,
            )
        onehot[...] = table

        @pl.loop(0, tiles // PREP_UNROLL)
        def _(q):
            for u in range(PREP_UNROLL):
                t = q * PREP_UNROLL + u
                base = pl.multiple_of(t * tile, tile)
                weights = wide_t[...] * onehot[pl.ds(t, 1), :]
                placed[pl.ds(base, tile), :] = weights.astype(jnp.bfloat16)
                total = band[t, 0].astype(jnp.float32)
                for o in range(1, 3):
                    total = total + band[t, o].astype(jnp.float32)
                for c in range(0, far_rows, LANE):
                    total = total + weights[:, c : c + LANE]
                degree = jnp.sum(total, axis=1, keepdims=True)
                seeded = jnp.broadcast_to(seed_ref[pl.ds(t, 1), :].astype(jnp.float32), (tile, tile)).T
                bound = jnp.broadcast_to(1.0 / (FLOOR * degree), (tile, tile))
                signed = jnp.where(seeded == 1.0, -bound, bound)
                limit[pl.ds(t * (tile // SUB), tile // SUB)] = signed.reshape(tile // SUB, SUB, tile)
                seeded = jnp.concatenate([seeded] * (WIDE // LANE), axis=1).astype(jnp.bfloat16)
                kept[pl.ds(t * (tile // GROUP), tile // GROUP)] = seeded.reshape(
                    tile // GROUP, GROUP, WIDE
                )

    copies = halo_first
    farw_copy.wait()
    band_copy.wait()
    prepare()
    lab_copy.wait()
    own_req.wait()
    pltpu.make_async_copy(req_s.at[others], req_s.at[others], req_recv).wait()
    exchange(0, 0)
    for it in range(ITERS):
        last = it == ITERS - 1
        band_inside(it)
        if it == 0:
            for c in range(1, CHUNKS):
                exchange(0, c)
            await_halo(it, copies)
            band_edges(it)
        for c in range(CHUNKS - 1):
            if it > 0:
                if c == 0:
                    await_factors()
                await_blocks(it, c)
                scale_received(it, c)
                if c == 0:
                    await_halo(it, copies)
                    band_edges(it)
            else:
                await_blocks(it, c)
            far_add(it, c)
            if not last:
                exchange(it + 1, c, raw=True)
        await_blocks(it, CHUNKS - 1)

        if not last:
            copies = halo_copies(
                it + 1, cur[it + 1].at[groups(tile, tile)], cur[it + 1].at[groups(rows, tile)]
            )

        def pair_at(i):
            return lax.rem(i + pairs - 1, pairs)

        far_pass(it, pair_at(0), far_a)

        @pl.loop(0, pairs // 2)
        def _(q):
            far_pass(it, pair_at(2 * q + 1), far_b)
            finish(it, pair_at(2 * q), far_a)
            far_pass(it, pair_at(2 * q + 2), far_a)
            finish(it, pair_at(2 * q + 1), far_b)
            if not last:

                @pl.when(q == 1)
                def _():
                    for copy in copies:
                        copy.start()

        if not last:
            exchange_factors()
            exchange(it + 1, CHUNKS - 1)

        sums = jnp.sum(part[...], axis=1)
        res_ref[it : it + 1, :] = jnp.sum(sums.T, axis=0, keepdims=True)

    sent = req_s.at[others]
    pltpu.make_async_copy(sent, sent, req_send).wait()


def body(labels, seed_mask, band_w, far_block, far_tile, far_count, far_w):
    rows, classes = labels.shape
    tiles, _, tile, _ = band_w.shape
    _, n, slots, blk, _ = far_w.shape
    per = slots * blk
    width = classes // CHUNKS
    dims = (n, tiles, tile, slots, blk, classes)
    vmem, anywhere = pltpu.VMEM, pl.BlockSpec(memory_space=pl.ANY)
    held = pl.BlockSpec(memory_space=pltpu.VMEM)
    dma = pltpu.SemaphoreType.DMA
    bf16, f32 = jnp.bfloat16, jnp.float32
    out, residual = pl.pallas_call(
        functools.partial(kernel, dims),
        out_shape=(
            pltpu.VMEM((rows // GROUP, GROUP, classes), bf16),
            jax.ShapeDtypeStruct((ITERS, tiles), f32),
        ),
        in_specs=[anywhere, anywhere, anywhere, held, held, held, held],
        out_specs=(held, held),
        scratch_shapes=[
            vmem(((rows + 2 * tile) // GROUP, GROUP, classes), bf16),
            vmem(((rows + 2 * tile) // GROUP, GROUP, classes), bf16),
            vmem(band_w.shape, bf16),
            vmem((n * per, tile), bf16),
            vmem((tile, n * per), f32),
            vmem((tiles, n * per), f32),
            vmem((rows, n * per), bf16),
            vmem((rows // SUB, SUB, classes), f32),
            vmem((2 * tile, width), f32),
            vmem((2 * tile, width), f32),
            vmem((rows // SUB, SUB, LANE), f32),
            vmem((rows // GROUP, GROUP, WIDE), bf16),
            vmem((rows // SUB, SUB, LANE), f32),
            vmem((tiles, 8, LANE), f32),
            vmem((2, tile // GROUP, GROUP, classes), bf16),
            vmem((2, tile // GROUP, GROUP, classes), bf16),
            vmem((ITERS, CHUNKS, n, per, width), bf16),
            vmem((ITERS, CHUNKS, n, per, width), bf16),
            vmem((n, 1, LANE), f32),
            vmem((n, 1, LANE), f32),
            pltpu.SMEM((n, slots, n), jnp.int32),
            dma, dma, dma, dma,
            dma, dma,
            dma((ITERS, 2)), dma((ITERS, 2)),
            dma((ITERS, CHUNKS)), dma((ITERS, CHUNKS)),
            dma, dma,
        ],
        compiler_params=pltpu.CompilerParams(
            collective_id=0, has_side_effects=True, vmem_limit_bytes=56 * 1024 * 1024
        ),
    )(
        labels.reshape(rows // GROUP, GROUP, classes),
        band_w,
        far_w.reshape(n * per, tile),
        far_block[0].T,
        far_tile[0].T,
        far_count,
        seed_mask.reshape(tiles, tile),
    )
    return out.reshape(rows, classes), residual


def solution(mesh):
    placed = (
        P("node", None),
        P("node"),
        P("node", None, None, None),
        P("node", None, None),
        P("node", None, None),
        P("node", None),
        P("node", None, None, None, None),
    )
    return jax.shard_map(
        body,
        mesh=mesh,
        in_specs=placed,
        out_specs=(P("node", None), P(None, "node")),
        check_vma=False,
    )
```

time: 54.7 us -> 47.4 us (0.87)
  the two profiles are of different devices: /device:TPU:29 before, /device:TPU:0 now
where the time goes in v1:
time: 47.4 us; the launch traced here: 47.2 us
  Pallas kernels  43.9 us (93%)
  local copies, waits for them, and re-layouts  2.58 us (5%)
  between operations  0.65 us (1%)
    pallas_call x1, Pallas kernels, body(): pl.pallas_call(functools.partial(kernel, dims), out_shape=(pltpu.VMEM((ro...  43.9 us
    unnamed x4, local copies, waits for them, and re-layouts  2.58 us

profile of v1, /device:TPU:0, one launch (start us, length us, event | category | flops | bytes accessed | tf_op | source)
XLA Modules:
  0.0 47.2 jit_solution(16273656501597701936)
XLA Ops:
  0.6 43.9 %shard_map.86 = (bf16[256,16,512]{2,1,0:T(8,128)(2,1)S(1)}, f32[2,32]{1,0:T(2,128)}) custom-call(bf16[256,16,512]{2,1,0:T(8,128)(2,1)} %bitcast.11, bf16[32,3,128,128]{3,2,1,0:T(8,128)(2,1)} %band_hbm.1, bf16[512,128]{1,0:T(8,128)(2,1)} %bitcast.12, s32[2,32]{1,0:T(2,128)} %bitcast.14, s32[2,32]{1,0:T(2,128)} %bitcast.15, s32[1,32]{1,0:T(1,128)} %count_ref.1, ...), custom_call_target="tpu_custom_call" | custom-call | tf_op jit(solution)/shard_map/pallas_call | solution.py:420
  44.6 0.0 copy-start
  44.6 2.0 %copy.11 = bf16[4096,512]{1,0:T(8,128)(2,1)} copy(bf16[4096,512]{1,0:T(8,128)(2,1)S(1)} %bitcast.10) | data formatting | bytes 8388608
  46.6 0.0 copy-done
  46.6 0.6 %copy.12 = f32[2,32]{1,0:T(2,128)} copy(f32[2,32]{1,0:T(2,128)S(1)} %copy-done) | data formatting | bytes 512
Async XLA Ops:
  44.6 2.0 %copy-start = (f32[2,32]{1,0:T(2,128)S(1)}, f32[2,32]{1,0:T(2,128)}, u32[]{:S(2)}) copy-start(f32[2,32]{1,0:T(2,128)} %get-tuple-element.11) | copy-start | bytes 772

commit v2 on v1

--- a/solution.py
+++ b/solution.py
@@ -17,18 +17,128 @@
 WIDE = 256
 FLOOR = 0.05
 BAND_UNROLL = 7
-FAR_UNROLL = 4
+NORM_UNROLL = 4
 SEND_UNROLL = 4
 SCALE_UNROLL = 16
+CLOSE_UNROLL = 4
+PEER_UNROLL = 6
 PREP_UNROLL = 4
+VMEM_BYTES = 62 * 1024 * 1024
+
+
+def finish_pair(p, pieces, acc, far, limit, fac, kept, old, old_at, new, new_at, part):
+    classes = acc.shape[2]
+    tile = pieces * ROWS // 2
+    for half in range(2):
+        total = jnp.zeros((8, LANE), jnp.float32)
+        for r in range(0, tile, ROWS):
+            row = half * tile + r
+            at8 = p * (2 * tile // SUB) + row // SUB
+            at16 = p * (2 * tile // GROUP) + row // GROUP
+            here8 = pl.ds(at8, ROWS // SUB)
+            here16 = pl.ds(at16, ROWS // GROUP)
+            before_at = pl.ds(at16 + old_at, ROWS // GROUP)
+            written = pl.ds(at16 + new_at, ROWS // GROUP)
+            local = slice(half * tile + r, half * tile + r + ROWS)
+            spread = []
+            for c in range(0, classes, WIDE):
+                value = acc[here8, :, c : c + WIDE].reshape(ROWS, WIDE)
+                if far is not None:
+                    start = classes - far.shape[1]
+                    if c >= start:
+                        value = value + far[local, c - start : c - start + WIDE]
+                spread.append(value)
+            if far is not None:
+                squares = spread[0] * spread[0]
+                for s in spread[1:]:
+                    squares = squares + s * s
+                mean = jnp.sum(squares, axis=1, keepdims=True) * (1.0 / classes)
+                signed = limit[here8].reshape(ROWS, LANE)
+                factor = jnp.minimum(lax.rsqrt(mean), jnp.abs(signed))
+            else:
+                factor = fac[here8].reshape(ROWS, LANE)
+            factor = jnp.concatenate([factor] * (WIDE // LANE), axis=1)
+            keep = kept[here16] > 0.5
+            moved = None
+            for q, s in enumerate(spread):
+                where = slice(q * WIDE, (q + 1) * WIDE)
+                before = old[before_at, :, where]
+                scaled = (s * factor).reshape(ROWS // GROUP, GROUP, WIDE)
+                fresh = jnp.where(keep, before, scaled.astype(jnp.bfloat16))
+                new[written, :, where] = fresh
+                change = jnp.abs(fresh - before)
+                moved = change if moved is None else moved + change
+            moved = moved.astype(jnp.float32).reshape(ROWS, WIDE)
+            for i in range(0, ROWS, 8):
+                for c in range(0, WIDE, LANE):
+                    total = total + moved[i : i + 8, c : c + LANE]
+        part[2 * p + half] = total
+
+
+def tile_sums(part):
+    sums = jnp.sum(part[...], axis=1)
+    return jnp.sum(sums.T, axis=0, keepdims=True)
+
+
+def closing(
+    dims,
+    acc, placed, coming, cur1, limit, kept, first_ref,
+    out_ref, res_ref,
+    far_a, far_b, staged, part, out_sem,
+):
+    tiles, tile = dims
+    pairs = tiles // 2
+    size = 2 * tile
+    far_rows, width = coming.shape[0] * coming.shape[1], coming.shape[2]
+
+    def far_pass(p, into):
+        into[...] = jnp.dot(
+            placed[pl.ds(pl.multiple_of(p * size, size), size), :],
+            coming[...].reshape(far_rows, width),
+            preferred_element_type=jnp.float32,
+        )
+
+    def finish(p, far):
+        finish_pair(
+            p, size // ROWS, acc, far, limit, None, kept, cur1, tile // GROUP, staged, 0, part
+        )
+
+    def out_copy(p):
+        here = pl.ds(p * (size // GROUP), size // GROUP)
+        return pltpu.make_async_copy(staged.at[here], out_ref.at[here], out_sem)
+
+    far_pass(0, far_a)
+    step = CLOSE_UNROLL if pairs % CLOSE_UNROLL == 0 else 2
+
+    @pl.loop(0, pairs // step)
+    def _(q):
+        for u in range(0, step, 2):
+            p = q * step + u
+            far_pass(p + 1, far_b)
+            finish(p, far_a)
+            after = p + 2
+            far_pass(after if u + 2 < step else jnp.where(after >= pairs, 0, after), far_a)
+            finish(p + 1, far_b)
+
+        @pl.when(q > 0)
+        def _():
+            out_copy(q * step - 1).start()
+
+        for u in range(step - 1):
+            out_copy(q * step + u).start()
+
+    res_ref[0:1, :] = first_ref[...]
+    res_ref[1:2, :] = tile_sums(part)
+    out_copy(pairs - 1).start()
+    pltpu.make_async_copy(staged, out_ref, out_sem).wait()
 
 
 def kernel(
     dims,
     labels_hbm, band_hbm, farw_hbm, req_ref, tile_ref, count_ref, seed_ref,
-    out_ref, res_ref,
-    cur0, cur1, band, farw, wide_t, onehot, placed, acc, far_a, far_b, limit, kept, fac, part,
-    halo0, halo1, send, recv, fac_out, fac_in, req_s,
+    acc, placed, coming, cur1, limit, kept, res_ref,
+    cur0, band, farw, wide_t, onehot, fac, part,
+    halo0, halo1, send, recv0, recv1, fac_out, fac_in, req_s,
     lab_sem, band_sem, farw_sem, smem_sem,
     req_send, req_recv, halo_send, halo_recv, blk_send, blk_recv, fac_send, fac_recv,
 ):
@@ -38,9 +148,16 @@
     far_rows = n * per
     width = classes // CHUNKS
     me = lax.axis_index("node")
-    right, left = lax.rem(me + 1, n), lax.rem(me + n - 1, n)
+
+    def around(index):
+        return jnp.where(index >= n, index - n, index)
+
+    right, left = around(me + 1), around(me + n - 1)
     cur = (cur0, cur1)
     halo = (halo0, halo1)
+    landing = {(0, c): recv0.at[c] for c in range(CHUNKS)}
+    landing.update({(1, c): recv1.at[c] for c in range(CHUNKS - 1)})
+    landing[1, CHUNKS - 1] = coming
     others = pl.ds(0, n - 1)
     pairs = tiles // 2
 
@@ -55,9 +172,21 @@
 
     barrier = pltpu.get_barrier_semaphore()
 
-    @pl.loop(1, n)
-    def _(j):
-        pl.semaphore_signal(barrier, inc=1, device_id=(lax.rem(me + j, n),), device_id_type=MESH)
+    def each_peer(act):
+        whole = (n - 1) // PEER_UNROLL
+
+        @pl.loop(0, whole)
+        def _(q):
+            for u in range(PEER_UNROLL):
+                act(around(me + q * PEER_UNROLL + u + 1))
+
+        for j in range(whole * PEER_UNROLL + 1, n):
+            act(around(me + j))
+
+    def greet(peer):
+        pl.semaphore_signal(barrier, inc=1, device_id=(peer,), device_id_type=MESH)
+
+    each_peer(greet)
 
     lab_copy = pltpu.make_async_copy(labels_hbm, cur0.at[groups(tile, rows)], lab_sem)
     band_copy = pltpu.make_async_copy(band_hbm, band, band_sem)
@@ -70,13 +199,13 @@
 
     pl.semaphore_wait(barrier, n - 1)
 
-    @pl.loop(1, n)
-    def _(j):
-        peer = lax.rem(me + j, n)
+    def ask(peer):
         pltpu.make_async_remote_copy(
             req_ref, req_s.at[me], req_send, req_recv,
             device_id=(peer,), device_id_type=MESH,
         ).start()
+
+    each_peer(ask)
 
     def halo_copies(it, low, high):
         return (
@@ -97,22 +226,23 @@
         copy.start()
 
     def block_copy(it, c, j):
-        peer = lax.rem(me + j, n)
+        peer = around(me + j)
         return pltpu.make_async_remote_copy(
-            send.at[it, c, peer], recv.at[it, c, me], blk_send.at[it, c], blk_recv.at[it, c],
+            send.at[it, c, peer], landing[it, c].at[me], blk_send.at[it, c], blk_recv.at[it, c],
             device_id=(peer,), device_id_type=MESH,
         )
 
     def factor_copy(j):
-        peer = lax.rem(me + j, n)
+        peer = around(me + j)
         return pltpu.make_async_remote_copy(
             fac_out.at[peer], fac_in.at[me], fac_send, fac_recv,
             device_id=(peer,), device_id_type=MESH,
         )
 
     def block_of(it, c, wanted):
-        pair = cur[it][wanted // 2 + tile // GROUP, :, columns(c)].astype(jnp.float32)
-        odd = jnp.full((blk, width), wanted % 2, jnp.int32) == 1
+        place = lax.shift_right_logical(wanted, 1) + tile // GROUP
+        pair = cur[it][place, :, columns(c)].astype(jnp.float32)
+        odd = jnp.full((blk, width), lax.bitwise_and(wanted, 1), jnp.int32) == 1
         return jnp.where(odd, pair[blk:], pair[:blk])
 
     def gathered(it, c, peer, raw):
@@ -132,7 +262,7 @@
         @pl.loop(0, n // SEND_UNROLL)
         def _(q):
             for u in range(SEND_UNROLL):
-                fill(lax.rem(me + q * SEND_UNROLL + u + 1, n))
+                fill(around(me + q * SEND_UNROLL + u + 1))
 
             @pl.when(q > 0)
             def _():
@@ -151,7 +281,7 @@
             return block_copy(it, c, j)
 
         send_all(fill, copy)
-        recv[it, c, me] = send[it, c, me]
+        landing[it, c][me] = send[it, c, me]
         send_rest(copy)
 
     diagonal = lax.broadcasted_iota(jnp.int32, (per, LANE), 0) == lax.broadcasted_iota(
@@ -181,9 +311,9 @@
         cur[it][groups(rows + tile, tile)] = halo[it][1]
 
     def await_blocks(it, c):
-        out_going, coming = send.at[it, c, others], recv.at[it, c, others]
-        pltpu.make_async_copy(out_going, out_going, blk_send.at[it, c]).wait()
-        pltpu.make_async_copy(coming, coming, blk_recv.at[it, c]).wait()
+        gone, came = send.at[it, c, others], landing[it, c].at[others]
+        pltpu.make_async_copy(gone, gone, blk_send.at[it, c]).wait()
+        pltpu.make_async_copy(came, came, blk_recv.at[it, c]).wait()
 
     def scale_received(it, c):
         @pl.loop(0, n // SCALE_UNROLL)
@@ -194,8 +324,8 @@
                     jnp.where(diagonal, jnp.broadcast_to(fac_in[s], (per, LANE)), 0.0),
                     axis=1, keepdims=True,
                 )
-                value = recv[it, c, s].astype(jnp.float32) * column
-                recv[it, c, s] = value.astype(jnp.bfloat16)
+                value = landing[it, c][s].astype(jnp.float32) * column
+                landing[it, c][s] = value.astype(jnp.bfloat16)
 
     def band_pairs(it, first, count):
         zero = jnp.zeros((tile, tile), jnp.bfloat16)
@@ -234,70 +364,60 @@
     def far_dot(it, c, start, size):
         return jnp.dot(
             placed[pl.ds(pl.multiple_of(start, size), size), :],
-            recv[it, c].reshape(far_rows, width),
+            landing[it, c][...].reshape(far_rows, width),
             preferred_element_type=jnp.float32,
         )
 
-    def far_add(it, c):
+    def far_pairs(it, c, first, count):
         size = 2 * tile
-
-        @pl.loop(0, pairs // FAR_UNROLL)
+        for u in range(count):
+            p = first + u
+            here = pl.ds(p * (size // SUB), size // SUB)
+            acc[here, :, columns(c)] += far_dot(it, c, p * size, size).reshape(
+                size // SUB, SUB, width
+            )
+
+    def far_inside(it, c):
+        @pl.loop(0, inner // unroll)
         def _(q):
-            for u in range(FAR_UNROLL):
-                p = q * FAR_UNROLL + u
-                here = pl.ds(p * (size // SUB), size // SUB)
-                acc[here, :, columns(c)] += far_dot(it, c, p * size, size).reshape(
-                    size // SUB, SUB, width
-                )
-
-    def far_pass(it, p, into):
-        into[...] = far_dot(it, CHUNKS - 1, p * (2 * tile), 2 * tile)
-
-    def finish(it, p, far):
-        last = it == ITERS - 1
-        target = out_ref if last else cur[1 - it]
-        for half in range(2):
-            total = jnp.zeros((8, LANE), jnp.float32)
-            for r in range(0, tile, ROWS):
-                row = p * (2 * tile) + half * tile + r
-                here8 = pl.ds(row // SUB, ROWS // SUB)
-                here16 = pl.ds(row // GROUP, ROWS // GROUP)
-                padded = pl.ds(row // GROUP + tile // GROUP, ROWS // GROUP)
-                local = slice(half * tile + r, half * tile + r + ROWS)
-                spread = []
-                for c in range(0, classes, WIDE):
-                    value = acc[here8, :, c : c + WIDE].reshape(ROWS, WIDE)
-                    start = (CHUNKS - 1) * width
-                    if c >= start:
-                        value = value + far[local, c - start : c - start + WIDE]
-                    spread.append(value)
-                squares = spread[0] * spread[0]
-                for s in spread[1:]:
-                    squares = squares + s * s
-                mean = jnp.sum(squares, axis=1, keepdims=True) * (1.0 / classes)
-                signed = limit[here8].reshape(ROWS, LANE)
-                factor = jnp.minimum(lax.rsqrt(mean), jnp.abs(signed))
-                if not last:
-                    fac[here8] = jnp.where(signed < 0.0, 1.0, factor).reshape(
-                        ROWS // SUB, SUB, LANE
-                    )
-                factor = jnp.concatenate([factor] * (WIDE // LANE), axis=1)
-                keep = kept[here16] > 0.5
-                written = here16 if last else padded
-                moved = None
-                for q, s in enumerate(spread):
-                    where = slice(q * WIDE, (q + 1) * WIDE)
-                    before = cur[it][padded, :, where]
-                    scaled = (s * factor).reshape(ROWS // GROUP, GROUP, WIDE)
-                    fresh = jnp.where(keep, before, scaled.astype(jnp.bfloat16))
-                    target[written, :, where] = fresh
-                    change = jnp.abs(fresh - before)
-                    moved = change if moved is None else moved + change
-                moved = moved.astype(jnp.float32).reshape(ROWS, WIDE)
-                for i in range(0, ROWS, 8):
-                    for c in range(0, WIDE, LANE):
-                        total = total + moved[i : i + 8, c : c + LANE]
-            part[2 * p + half] = total
+            far_pairs(it, c, q * unroll + 1, unroll)
+
+    def far_edges(it, c):
+        far_pairs(it, c, 0, 1)
+        far_pairs(it, c, pairs - 1, 1)
+
+    def norm_pairs(it, first, count):
+        size = 2 * tile
+        c = CHUNKS - 1
+        for u in range(count):
+            p = first + u
+            here = pl.ds(p * (size // SUB), size // SUB)
+            value = far_dot(it, c, p * size, size)
+            value = value + acc[here, :, columns(c)].reshape(size, width)
+            acc[here, :, columns(c)] = value.reshape(size // SUB, SUB, width)
+            squares = value * value
+            for other in range(CHUNKS - 1):
+                value = acc[here, :, columns(other)].reshape(size, width)
+                squares = squares + value * value
+            mean = jnp.sum(squares, axis=1, keepdims=True) * (1.0 / classes)
+            signed = limit[here].reshape(size, LANE)
+            factor = jnp.minimum(lax.rsqrt(mean), jnp.abs(signed))
+            fac[here] = jnp.where(signed < 0.0, 1.0, factor).reshape(size // SUB, SUB, LANE)
+
+    def norm_inside(it):
+        @pl.loop(0, inner // unroll)
+        def _(q):
+            norm_pairs(it, q * unroll + 1, unroll)
+
+    def norm_edges(it):
+        norm_pairs(it, 0, 1)
+        norm_pairs(it, pairs - 1, 1)
+
+    def finish(p):
+        finish_pair(
+            p, 2 * tile // ROWS, acc, None, limit, fac, kept, cur0, tile // GROUP,
+            cur1, tile // GROUP, part,
+        )
 
     def prepare():
         wide_t[...] = farw[...].astype(jnp.float32).T
@@ -348,60 +468,46 @@
     own_req.wait()
     pltpu.make_async_copy(req_s.at[others], req_s.at[others], req_recv).wait()
     exchange(0, 0)
-    for it in range(ITERS):
-        last = it == ITERS - 1
-        band_inside(it)
-        if it == 0:
-            for c in range(1, CHUNKS):
-                exchange(0, c)
-            await_halo(it, copies)
-            band_edges(it)
-        for c in range(CHUNKS - 1):
-            if it > 0:
-                if c == 0:
-                    await_factors()
-                await_blocks(it, c)
-                scale_received(it, c)
-                if c == 0:
-                    await_halo(it, copies)
-                    band_edges(it)
-            else:
-                await_blocks(it, c)
-            far_add(it, c)
-            if not last:
-                exchange(it + 1, c, raw=True)
-        await_blocks(it, CHUNKS - 1)
-
-        if not last:
-            copies = halo_copies(
-                it + 1, cur[it + 1].at[groups(tile, tile)], cur[it + 1].at[groups(rows, tile)]
-            )
-
-        def pair_at(i):
-            return lax.rem(i + pairs - 1, pairs)
-
-        far_pass(it, pair_at(0), far_a)
-
-        @pl.loop(0, pairs // 2)
-        def _(q):
-            far_pass(it, pair_at(2 * q + 1), far_b)
-            finish(it, pair_at(2 * q), far_a)
-            far_pass(it, pair_at(2 * q + 2), far_a)
-            finish(it, pair_at(2 * q + 1), far_b)
-            if not last:
-
-                @pl.when(q == 1)
-                def _():
-                    for copy in copies:
-                        copy.start()
-
-        if not last:
-            exchange_factors()
-            exchange(it + 1, CHUNKS - 1)
-
-        sums = jnp.sum(part[...], axis=1)
-        res_ref[it : it + 1, :] = jnp.sum(sums.T, axis=0, keepdims=True)
-
+    final = CHUNKS - 1
+
+    band_inside(0)
+    for c in range(1, CHUNKS):
+        exchange(0, c)
+    await_halo(0, copies)
+    band_edges(0)
+    for c in range(final):
+        await_blocks(0, c)
+        far_inside(0, c)
+        far_edges(0, c)
+        exchange(1, c, raw=True)
+    await_blocks(0, final)
+    norm_edges(0)
+    finish(0)
+    finish(pairs - 1)
+    copies = halo_copies(1, cur[1].at[groups(tile, tile)], cur[1].at[groups(rows, tile)])
+    norm_inside(0)
+    exchange_factors()
+    for copy in copies:
+        copy.start()
+    exchange(1, final, raw=True)
+
+    @pl.loop(1, pairs - 1)
+    def _(p):
+        finish(p)
+
+    res_ref[...] = tile_sums(part)
+    band_inside(1)
+    await_factors()
+    for c in range(final):
+        await_blocks(1, c)
+        scale_received(1, c)
+        far_inside(1, c)
+    await_halo(1, copies)
+    band_edges(1)
+    for c in range(final):
+        far_edges(1, c)
+    await_blocks(1, final)
+    scale_received(1, final)
     sent = req_s.at[others]
     pltpu.make_async_copy(sent, sent, req_send).wait()
 
@@ -417,33 +523,34 @@
     held = pl.BlockSpec(memory_space=pltpu.VMEM)
     dma = pltpu.SemaphoreType.DMA
     bf16, f32 = jnp.bfloat16, jnp.float32
-    out, residual = pl.pallas_call(
+    passed_on = 4 * rows * (classes + LANE)
+    passed_on += 2 * (rows * (n * per + WIDE) + n * per * width + (rows + 2 * tile) * classes)
+    *kept_in_vmem, first = pl.pallas_call(
         functools.partial(kernel, dims),
         out_shape=(
-            pltpu.VMEM((rows // GROUP, GROUP, classes), bf16),
-            jax.ShapeDtypeStruct((ITERS, tiles), f32),
+            vmem((rows // SUB, SUB, classes), f32),
+            vmem((rows, n * per), bf16),
+            vmem((n, per, width), bf16),
+            vmem(((rows + 2 * tile) // GROUP, GROUP, classes), bf16),
+            vmem((rows // SUB, SUB, LANE), f32),
+            vmem((rows // GROUP, GROUP, WIDE), bf16),
+            vmem((1, tiles), f32),
         ),
         in_specs=[anywhere, anywhere, anywhere, held, held, held, held],
-        out_specs=(held, held),
+        out_specs=(held,) * 7,
         scratch_shapes=[
-            vmem(((rows + 2 * tile) // GROUP, GROUP, classes), bf16),
             vmem(((rows + 2 * tile) // GROUP, GROUP, classes), bf16),
             vmem(band_w.shape, bf16),
             vmem((n * per, tile), bf16),
             vmem((tile, n * per), f32),
             vmem((tiles, n * per), f32),
-            vmem((rows, n * per), bf16),
-            vmem((rows // SUB, SUB, classes), f32),
-            vmem((2 * tile, width), f32),
-            vmem((2 * tile, width), f32),
-            vmem((rows // SUB, SUB, LANE), f32),
-            vmem((rows // GROUP, GROUP, WIDE), bf16),
             vmem((rows // SUB, SUB, LANE), f32),
             vmem((tiles, 8, LANE), f32),
             vmem((2, tile // GROUP, GROUP, classes), bf16),
             vmem((2, tile // GROUP, GROUP, classes), bf16),
             vmem((ITERS, CHUNKS, n, per, width), bf16),
-            vmem((ITERS, CHUNKS, n, per, width), bf16),
+            vmem((CHUNKS, n, per, width), bf16),
+            vmem((CHUNKS - 1, n, per, width), bf16),
             vmem((n, 1, LANE), f32),
             vmem((n, 1, LANE), f32),
             pltpu.SMEM((n, slots, n), jnp.int32),
@@ -454,7 +561,8 @@
             dma, dma,
         ],
         compiler_params=pltpu.CompilerParams(
-            collective_id=0, has_side_effects=True, vmem_limit_bytes=56 * 1024 * 1024
+            collective_id=0, has_side_effects=True,
+            vmem_limit_bytes=VMEM_BYTES - passed_on,
         ),
     )(
         labels.reshape(rows // GROUP, GROUP, classes),
@@ -465,6 +573,23 @@
         far_count,
         seed_mask.reshape(tiles, tile),
     )
+    out, residual = pl.pallas_call(
+        functools.partial(closing, (tiles, tile)),
+        out_shape=(
+            jax.ShapeDtypeStruct((rows // GROUP, GROUP, classes), bf16),
+            jax.ShapeDtypeStruct((ITERS, tiles), f32),
+        ),
+        in_specs=[held] * 7,
+        out_specs=(anywhere, held),
+        scratch_shapes=[
+            vmem((2 * tile, width), f32),
+            vmem((2 * tile, width), f32),
+            vmem((rows // GROUP, GROUP, classes), bf16),
+            vmem((tiles, 8, LANE), f32),
+            dma,
+        ],
+        compiler_params=pltpu.CompilerParams(vmem_limit_bytes=12 * 1024 * 1024),
+    )(*kept_in_vmem, first)
     return out.reshape(rows, classes), residual
 
 

time: 47.4 us -> 44 us (0.928)
  local copies, waits for them, and re-layouts: 2.58 us -> 0 us
  Pallas kernels: 43.9 us -> 43.1 us
    unnamed x4 -> x0, local copies, waits for them, and re-layouts: 2.58 us -> none
    pallas_call x1 -> x2, Pallas kernels: 43.9 us -> 43.1 us  [the longest x1 38.3 us: body(): pl.pallas_call(functools.partial(kernel, dims), out_shape=(vmem((rows //...]
where the time goes in v2:
time: 44 us; the launch traced here: 43.7 us
  Pallas kernels  43.1 us (98%)
  between operations  0.64 us (1%)
    pallas_call x1, Pallas kernels, body(): pl.pallas_call(functools.partial(kernel, dims), out_shape=(vmem((rows //...  38.3 us
    pallas_call x1, Pallas kernels, body(): pl.pallas_call(functools.partial(closing, (tiles, tile)), out_shape=(jax....  4.84 us

profile of v2, /device:TPU:0, one launch (start us, length us, event | category | flops | bytes accessed | tf_op | source)
XLA Modules:
  0.0 43.7 jit_solution(4488595089321599803)
XLA Ops:
  0.6 38.3 %shard_map.86 = (f32[512,8,512]{2,1,0:T(8,128)S(1)}, bf16[4096,512]{1,0:T(8,128)(2,1)S(1)}, bf16[32,16,256]{2,1,0:T(8,128)(2,1)S(1)}, bf16[272,16,512]{2,1,0:T(8...) custom-call(bf16[256,16,512]{2,1,0:T(8,128)(2,1)} %bitcast.10, ...), custom_call_target="tpu_custom_call" | custom-call | tf_op jit(solution)/shard_map/pallas_call | solution.py:528
  38.9 4.8 %shard_map.87 = (bf16[256,16,512]{2,1,0:T(8,128)(2,1)}, f32[2,32]{1,0:T(2,128)}) custom-call(f32[512,8,512]{2,1,0:T(8,128)S(1)} %get-tuple-element.11.acc, bf16[4096,512]{1,0:T(8,128)(2,1)S(1)} %get-tuple-element.12.placed, bf16[32,16,256]{2,1,0:T(8,128)(2,1)S(1)} %get-tuple-element.13.coming, bf16[272,16,512]{2,1,0:T(8,128)(2,1)S(1)} %get-tuple-element.14.cur1, ...), custom_call_target="tpu_custom_call" | custom-call | tf_op jit(solution)/shard_map/pallas_call | solution.py:576
